TPU v7x, 256 devices: a 2x2x32 block of a 4x8x32 slice. The times are simulated.
256 devices in a mesh: groups: 4 (over y, x), asset: 64 (over z, core).
Axes of the slice: x: 2, y: 2, z: 32, core: 2. Of those that a mesh axis runs over, the one named last changes fastest.
The devices are a block of a 4x8x32 slice.
Arguments:
- scen_draws: bfloat16 [16384, 256], P(('groups', 'asset')), parts along dimension 0, may hold values from -4 to 4
- factor_mix: bfloat16 [256, 256], replicated, may hold values from -0.375 to 0.375
- loadings: bfloat16 [262144, 256], P(('groups', 'asset')), parts along dimension 0, may hold values from -0.375 to 0.375
- convexity: float32 [262144], P(('groups', 'asset')), parts along dimension 0, may hold values from -0.6 to 0.6
- holdings: float32 [262144], P(('groups', 'asset')), parts along dimension 0, may hold values from -0.110485435 to 0.110485435
- desk_map: int32 [262144], P(('groups', 'asset')), parts along dimension 0, may hold values from 0 to 127
- ranks: int32 [16384], P('groups'), parts along dimension 0, may hold values from 0 to 4095, each once
- desk_prices: float32 [512], P('groups'), parts along dimension 0, may hold values from -5 to 5
Outputs:
- allocation: float32 [512], P('groups'), parts along dimension 0
- grad_loadings: float32 [262144, 256], P(('groups', 'asset')), parts along dimension 0
- grad_convexity: float32 [262144], P(('groups', 'asset')), parts along dimension 0
There are 4 independent parts, one for each index of `groups`. A program takes and returns all parts, laid end to end along the dimension named above; an argument that names none is the same for every part. Nothing has to cross between parts.
All inputs are finite; a program needn't handle non-finite values.
Results may differ from a plain program's by a relative error of at most 0.0029.
Values may be sent and summed in bfloat16 or wider, within the bound.
No kernel may reach another device: no remote copies, remote signals or barrier semaphores. Data moves between devices by JAX's collectives and lax.ppermute only.
A program may use at most 64 MiB of HBM per device.

v0:
```python
import math
import jax
import jax.numpy as jnp
from jax import lax
from jax.sharding import Mesh
from jax.sharding import PartitionSpec as P

DESKS = 128
BAND = 32
CENTER = 166
ASSET = ("asset_0", "asset_1")
GROUPS_ASSET = ("groups", "asset_0", "asset_1")


def filled_up(lines, size):
    spare = -lines.shape[0] % size
    if not spare:
        return lines
    return jnp.concatenate([lines, jnp.zeros((spare, *lines.shape[1:]), lines.dtype)])


def copy_for_each(x, axis):
    copies = jnp.broadcast_to(x, (lax.axis_size(axis), *x.shape))
    return lax.all_to_all(copies, axis, split_axis=0, concat_axis=0, tiled=True)


def laid_out(tiles, dim):
    tiles = jnp.moveaxis(tiles, 0, dim)
    shape = tiles.shape
    return tiles.reshape(*shape[:dim], shape[dim] * shape[dim + 1], *shape[dim + 2 :])


def collect(x, axis, dim):
    tiles = copy_for_each(x, axis)
    return laid_out(tiles, dim)


def cut_along(x, dim, size):
    before, after = (x.shape[:dim], x.shape[dim + 1 :])
    return jnp.moveaxis(x.reshape(*before, size, -1, *after), dim, 0)


def summed_on_arrival(x, axis, dim):
    size = lax.axis_size(axis)
    tiles = lax.all_to_all(cut_along(x, dim, size), axis, 0, 0, tiled=True)
    return jnp.sum(tiles, axis=0)


def total_of(x, axes):
    padded = filled_up(x, lax.axis_size(axes))
    whole = collect(summed_on_arrival(padded, axes, 0), axes, 0)
    return lax.slice_in_dim(whole, 0, len(x)).reshape(x.shape)


def packed_total(arrays, axis):
    ends = [0]
    for a in arrays:
        ends.append(ends[-1] + a.size)
    running = total_of(jnp.concatenate([a.ravel() for a in arrays]), axis)
    return tuple((running[b:e].reshape(a.shape) for a, b, e in zip(arrays, ends, ends[1:])))


def over_axes(x, axes):
    for axis in axes:
        x = lax.psum(x, axis)
    return x


def gather_axes(x, axes, dim):
    far, near = axes
    first = copy_for_each(x, far)
    tiles = jnp.swapaxes(copy_for_each(first, near), 0, 1)
    return laid_out(tiles.reshape(-1, *x.shape), dim)


def smooth_bend(value):
    return jnp.logaddexp(value, -value) - math.log(2.0)


def rank_kernel(ranks, scenarios):
    centre = jnp.float32(CENTER)
    spread = jnp.float32(BAND)
    offsets = (ranks.astype(jnp.float32) - centre) / spread
    every = (jnp.arange(scenarios, dtype=jnp.float32) - centre) / spread
    return jnp.exp(-0.5 * offsets * offsets) / jnp.sum(jnp.exp(-0.5 * every * every))


def cotangent_of(
    weights,
    weight_total,
    slopes,
    smoothing,
    kernel,
    grad_quant,
    grad_band,
    centred,
    prices,
    scenarios,
):
    grad_loss = (
        slopes / smoothing
        + kernel * grad_quant
        + grad_band * 0.09 * centred / (scenarios * smoothing)
    )
    return (
        scenarios * (-weights[:, None] * prices[None, :] / weight_total - grad_loss[:, None])
    ).astype(jnp.bfloat16)


def tail_core(losses, valued, ranks, prices):
    scenarios = losses.shape[0]
    kernel = rank_kernel(ranks, scenarios)
    quantile = jnp.sum(kernel * losses)
    average = jnp.mean(losses)
    centred = losses - average
    smoothing = 0.3 * jnp.sqrt(jnp.mean(centred * centred) + 1e-06)
    scores = (losses - quantile) / smoothing
    weights = jax.nn.sigmoid(scores)
    weight_total = jnp.sum(weights)
    objective = -jnp.sum(weights * valued) / weight_total
    slopes = (-valued - objective) / weight_total * weights * (1.0 - weights)
    grad_quant = -jnp.sum(slopes) / smoothing
    grad_band = -jnp.sum(slopes * scores) / smoothing
    cotangent = cotangent_of(
        weights,
        weight_total,
        slopes,
        smoothing,
        kernel,
        grad_quant,
        grad_band,
        centred,
        prices,
        scenarios,
    )
    return (cotangent, weights, weight_total)


def tail_columns(partial_value, ranks, prices):
    sums = packed_total(
        (-jnp.sum(partial_value, axis=1), jnp.sum(partial_value * prices[None, :], axis=1)), ASSET
    )
    cotangent, weights, weight_total = tail_core(sums[0], sums[1], ranks, prices)
    weighted = over_axes(jnp.sum(weights[:, None] * partial_value, axis=0), ASSET)
    return (cotangent, -weighted / weight_total)


def desk_table(desk_map):
    columns = jnp.arange(DESKS, dtype=jnp.int32)
    return (desk_map[:, None] == columns[None, :]).astype(jnp.bfloat16)


def split_rows(array, block_rows):
    return array.reshape((-1, block_rows) + array.shape[1:])


def exposure_of(shock_rows, loadings):
    return lax.dot_general(
        shock_rows, loadings, (((1,), (1,)), ((), ())), preferred_element_type=jnp.float32
    )


def pnl_rows(shock_rows, loadings, convexity, holdings, table):
    number = shock_rows.shape[0]
    block_rows = math.gcd(number, 512)

    def pnl_one_block(shock_block):
        exposure = exposure_of(shock_block, loadings)
        held = (holdings * (exposure + convexity * smooth_bend(exposure))).astype(jnp.bfloat16)
        return jnp.dot(held, table, preferred_element_type=jnp.float32)

    result = lax.map(pnl_one_block, split_rows(shock_rows, block_rows))
    return result.reshape((number, table.shape[1]))


def grad_rows(carry, shock_rows, cot_rows, loadings, convexity, holdings, table):
    number = shock_rows.shape[0]
    block_rows = math.gcd(number, 512)

    def grad_one_block(state, inputs):
        shock_block, cot_block = inputs
        exposure = exposure_of(shock_block, loadings)
        spread_back = lax.dot_general(
            cot_block, table, (((1,), (1,)), ((), ())), preferred_element_type=jnp.float32
        )
        held = holdings * spread_back
        grad_exposure = (held * (1.0 + convexity * jnp.tanh(exposure))).astype(jnp.bfloat16)
        grad_load = state[0] + lax.dot_general(
            grad_exposure, shock_block, (((0,), (0,)), ((), ())), preferred_element_type=jnp.float32
        )
        grad_conv = state[1] + jnp.sum(held * smooth_bend(exposure), axis=0)
        return ((grad_load, grad_conv), None)

    final, ignored = lax.scan(
        grad_one_block,
        carry,
        (split_rows(shock_rows, block_rows), split_rows(cot_rows, block_rows)),
    )
    return final


def shards(scen_draws, factor_mix, loadings, convexity, holdings, desk_map, ranks, desk_prices):
    local_shocks = jnp.dot(scen_draws, factor_mix, preferred_element_type=jnp.float32).astype(
        jnp.bfloat16
    )
    table = desk_table(desk_map)
    shocks = gather_axes(local_shocks, ("asset_0", "asset_1"), 0)
    partial_value = pnl_rows(shocks, loadings, convexity, holdings, table)
    cotangent, allocation = tail_columns(partial_value, ranks, desk_prices)
    initial = (
        jnp.zeros((loadings.shape[0], loadings.shape[1]), jnp.float32),
        jnp.zeros((loadings.shape[0],), jnp.float32),
    )
    grad_load, grad_conv = grad_rows(
        initial, shocks, cotangent, loadings, convexity, holdings, table
    )
    squares = over_axes(jnp.sum(grad_load * grad_load) + jnp.sum(grad_conv * grad_conv), ASSET)
    entries = loadings.shape[0] * lax.axis_size(ASSET) * (loadings.shape[1] + 1)
    factor = lax.rsqrt(squares / entries + 1e-06)
    return (allocation, grad_load * factor, grad_conv * factor)


def solution(mesh):
    torus = Mesh(
        mesh.devices.reshape(mesh.shape["groups"], 32, 2), ("groups", "asset_0", "asset_1")
    )
    return jax.shard_map(
        shards,
        mesh=torus,
        in_specs=(
            P(GROUPS_ASSET, None),
            P(),
            P(GROUPS_ASSET, None),
            P(GROUPS_ASSET),
            P(GROUPS_ASSET),
            P(GROUPS_ASSET),
            P("groups"),
            P("groups"),
        ),
        out_specs=(P("groups"), P(GROUPS_ASSET, None), P(GROUPS_ASSET)),
        check_vma=False,
    )
```

profile of v0, /device:TPU:37, one launch (start us, length us, event | category | flops | bytes accessed | tf_op | source)
XLA Modules:
  0.0 359.4 jit_solution(15060804531510212304)
XLA Ops:
  3.5 33.2 %all-to-all-start = ((bf16[32,64,256]{2,1,0:T(8,128)(2,1)}), bf16[32,64,256]{2,1,0:T(8,128)(2,1)S(1)}, u32[]{:S(2)}, u32[]{:S(2)}) async-start(bf16[32,64,256]{2,1,0:T(8,128)(2,1)} %broadcast_in_dim.37), calls=%async_computation | async-start | bytes 2097152 | tf_op jit(solution)/shard_map/all_to_all | solution.py:24
  36.8 104.4 %all-to-all-done = bf16[32,64,256]{2,1,0:T(8,128)(2,1)S(1)} async-done(((bf16[32,64,256]{2,1,0:T(8,128)(2,1)}), bf16[32,64,256]{2,1,0:T(8,128)(2,1)S(1)}, u32[]{:S(2)}, u32[]{:S(2)}) %all-to-all-start) | async-done | bytes 1048608 | tf_op jit(solution)/shard_map/all_to_all | solution.py:24
  141.4 6.0 %all_to_all.25 = bf16[2,32,64,256]{3,2,1,0:T(8,128)(2,1)S(1)} all-to-all(bf16[2,32,64,256]{3,2,1,0:T(8,128)(2,1)S(1)} %broadcast_in_dim.38), channel_id=1, replica_groups=mesh['groups'=4,'asset_0'=32,'asset_1'=2] {'asset_1'}, dimensions={0} | all-to-all | bytes 4194304 | tf_op jit(solution)/shard_map/all_to_all | solution.py:24
  149.0 23.4 %while.28 = (s32[]{:T(128)}, f32[8,512,128]{2,1,0:T(8,128)S(1)}, f32[1024]{0:T(1024)S(1)}, bf16[8,512,256]{2,1,0:T(8,128)(2,1)}, bf16[1024,256]{1,0:T(8,128)(2,1...) while((s32[]{:T(128)}, f32[8,512,128]{2,1,0:T(8,128)S(1)}, f32[1024]{0:T(1024)S(1)}, ...), condition=%wide.region_1.2_spmd.clone, body=%wide.region_0.1_spmd.clone.sunk | while | flops 410255360 | bytes 1061981 | solution.py:172
  149.0 2.9 fusion.83
  151.9 2.9 fusion.83
  154.8 2.9 fusion.83
  157.7 2.9 fusion.83
  160.7 2.9 fusion.83
  163.6 2.9 fusion.83
  166.5 2.9 fusion.83
  169.4 2.9 fusion.83
  173.6 30.4 %all_to_all.26 = f32[64,1,128]{2,1,0:T(1,128)S(1)} all-to-all(f32[64,1,128]{2,1,0:T(1,128)S(1)} %bitcast.91), channel_id=1, replica_groups=mesh['groups'=4,'asset_0'=32,'asset_1'=2] {'asset_0','asset_1'}, dimensions={0} | all-to-all | bytes 65536 | tf_op jit(solution)/shard_map/all_to_all | solution.py:45
  204.7 6.3 %all-to-all-start.3 = ((f32[64,1,128]{2,1,0:T(1,128)}), f32[64,1,128]{2,1,0:T(1,128)S(1)}, u32[]{:S(2)}, u32[]{:S(2)}) async-start(f32[64,1,128]{2,1,0:T(1,128)} %broadcast_in_dim.39), calls=%async_computation.3 | async-start | bytes 65536 | tf_op jit(solution)/shard_map/all_to_all | solution.py:24
  211.6 22.0 %all-to-all-done.3 = f32[64,1,128]{2,1,0:T(1,128)S(1)} async-done(((f32[64,1,128]{2,1,0:T(1,128)}), f32[64,1,128]{2,1,0:T(1,128)S(1)}, u32[]{:S(2)}, u32[]{:S(2)}) %all-to-all-start.3) | async-done | bytes 32800 | tf_op jit(solution)/shard_map/all_to_all | solution.py:24
  248.6 47.0 %while.29 = (s32[]{:T(128)}, f32[1024,256]{1,0:T(8,128)S(1)}, f32[1024]{0:T(1024)S(1)}, f32[1024]{0:T(1024)S(1)}, bf16[8,512,128]{2,1,0:T(8,128)(2,1)S(1)}, /*in...) while((s32[]{:T(128)}, f32[1024,256]{1,0:T(8,128)S(1)}, ...), condition=%wide.region_18.19_spmd.clone, body=%wide.region_16.18_spmd.clone.sunk | while | flops 681313280 | bytes 15892648 | solution.py:194
  249.6 2.8 fusion.89
  255.5 2.8 fusion.89
  258.3 2.0 convolution_add_fusion.2
  261.4 2.8 fusion.89
  264.2 2.0 convolution_add_fusion.2
  267.3 2.8 fusion.89
  270.0 2.0 convolution_add_fusion.2
  273.2 2.8 fusion.89
  275.9 2.0 convolution_add_fusion.2
  279.0 2.8 fusion.89
  281.8 2.0 convolution_add_fusion.2
  284.9 2.8 fusion.89
  287.7 2.0 convolution_add_fusion.2
  290.8 2.8 fusion.89
  298.4 40.2 %all-reduce = (f32[128]{0:T(128)S(1)}, f32[]{:T(128)}) all-reduce(f32[128]{0:T(128)S(1)} %multiply_reduce_fusion, f32[]{:T(128)S(6)} %add.117), channel_id=1, replica_groups=mesh['groups'=4,'asset_0'=32,'asset_1'=2] {'asset_0'}, use_global_device_ids=true, to_apply=%region_10.11 | all-reduce | flops 129 | bytes 1032 | tf_op jit(solution)/shard_map/psum | solution.py:65
  338.6 17.4 %all-reduce.1 = (f32[128]{0:T(128)S(1)}, f32[]{:T(128)}) all-reduce(f32[128]{0:T(128)S(1)} %get-tuple-element.297, f32[]{:T(128)} %get-tuple-element.298), channel_id=1, replica_groups=mesh['groups'=4,'asset_0'=32,'asset_1'=2] {'asset_1'}, use_global_device_ids=true, to_apply=%region_11.12 | all-reduce | flops 129 | bytes 1032 | tf_op jit(solution)/shard_map/psum | solution.py:65
  (82 shorter events, 34.6 us)
Async XLA Ops:
  0.6 0.9 copy-start
  3.5 137.7 %all-to-all-start = ((bf16[32,64,256]{2,1,0:T(8,128)(2,1)}), bf16[32,64,256]{2,1,0:T(8,128)(2,1)S(1)}, u32[]{:S(2)}, u32[]{:S(2)}) async-start(bf16[32,64,256]{2,1,0:T(8,128)(2,1)} %broadcast_in_dim.37), calls=%async_computation | async-start | bytes 2097152 | tf_op jit(solution)/shard_map/all_to_all | solution.py:24
  147.4 1.5 copy-start.1
  147.4 1.5 copy-start.2
  147.4 1.5 copy-start.3
  147.4 1.5 copy-start.6
  148.9 23.4 %copy-start.5 = (f32[128]{0:T(128)S(1)}, f32[128]{0:T(128)}, u32[]{:S(2)}) copy-start(f32[128]{0:T(128)} %param.19) | copy-start | bytes 1540
  172.4 63.9 %copy-start.4 = (s32[4096]{0:T(1024)S(1)}, s32[4096]{0:T(1024)}, u32[]{:S(2)}) copy-start(s32[4096]{0:T(1024)} %param.18) | copy-start | bytes 49156
  204.7 28.9 %all-to-all-start.3 = ((f32[64,1,128]{2,1,0:T(1,128)}), f32[64,1,128]{2,1,0:T(1,128)S(1)}, u32[]{:S(2)}, u32[]{:S(2)}) async-start(f32[64,1,128]{2,1,0:T(1,128)} %broadcast_in_dim.39), calls=%async_computation.3 | async-start | bytes 65536 | tf_op jit(solution)/shard_map/all_to_all | solution.py:24
  248.6 1.0 copy-start.7
  254.5 1.0 copy-start.7
  260.4 1.0 copy-start.7
  266.2 1.0 copy-start.7
  272.1 1.0 copy-start.7
  278.0 1.0 copy-start.7
  283.9 1.0 copy-start.7
  289.7 1.0 copy-start.7
where the time goes:
time: 361 us; the launch traced here: 359 us
  waiting for transfers between devices  126 us (35%)
  blocking collectives  94 us (26%)
  matrix products  66.8 us (19%)
  starting transfers between devices  39.5 us (11%)
  other arithmetic  17 us (5%)
  local copies, waits for them, and re-layouts  8.24 us (2%)
  between operations  6.85 us (2%)
    all_to_all x2, waiting for transfers between devices, copy_for_each(): return lax.all_to_all(copies, axis, split_axis=0, concat_axis=0, tiled=True)  126 us
    psum x2, blocking collectives, over_axes(): x = lax.psum(x, axis)  57.6 us
    all_to_all x2, starting transfers between devices, copy_for_each(): return lax.all_to_all(copies, axis, split_axis=0, concat_axis=0, tiled=True)  39.5 us
    all_to_all x1, blocking collectives, summed_on_arrival(): tiles = lax.all_to_all(cut_along(x, dim, size), axis, 0, 0, tiled=True)  30.4 us
    dot_general x8, matrix products, pnl_one_block(): return jnp.dot(held, table, preferred_element_type=jnp.float32)  23.2 us
    dot_general x8, matrix products, exposure_of(): lax.dot_general(shock_rows, loadings, (((1,), (1,)), ((), ())), preferred...  22.1 us
    dot_general x8, matrix products, grad_one_block(): lax.dot_general(grad_exposure, shock_block, (((0,), (0,)), ((), ())), pre...  16.3 us
  transfers between devices with their start and end apart: 2, of which 2 were waited for; matrix products, arithmetic and copies ran while one was open for 0% of the time, Pallas kernels for 0%

commit v1 on v0

--- a/solution.py
+++ b/solution.py
@@ -62,7 +62,7 @@
 
 def over_axes(x, axes):
     for axis in axes:
-        x = lax.psum(x, axis)
+        x = jnp.sum(lax.all_gather(x, axis), axis=0)
     return x
 
 

time: 361 us -> 438 us (1.21)
  blocking collectives: 94 us -> 147 us
  matrix products: 66.8 us -> 89.3 us
    psum x2 -> x0, blocking collectives: 57.6 us -> none  [over_axes(): x = lax.psum(x, axis)]
    unnamed x0 -> x2, blocking collectives: none -> 56.5 us
    all_gather x0 -> x2, blocking collectives: none -> 54.5 us  [over_axes(): x = jnp.sum(lax.all_gather(x, axis), axis=0)]
    dot_general x8, matrix products: 22.1 us -> 32 us  [exposure_of(): lax.dot_general(shock_rows, loadings, (((1,), (1,)), ((), ())), preferred...]
    dot_general x8, matrix products: 4.4 us -> 12.1 us  [grad_one_block(): lax.dot_general(cot_block, table, (((1,), (1,)), ((), ())), preferred_ele...]
    dot_general x8, matrix products: 16.3 us -> 21.1 us  [grad_one_block(): lax.dot_general(grad_exposure, shock_block, (((0,), (0,)), ((), ())), pre...]
where the time goes in v1:
time: 438 us; the launch traced here: 437 us
  blocking collectives  147 us (34%)
  waiting for transfers between devices  125 us (29%)
  matrix products  89.3 us (20%)
  starting transfers between devices  39.5 us (9%)
  other arithmetic  20.1 us (5%)
  local copies, waits for them, and re-layouts  7.89 us (2%)
  between operations  6.86 us (2%)
    all_to_all x2, waiting for transfers between devices, copy_for_each(): return lax.all_to_all(copies, axis, split_axis=0, concat_axis=0, tiled=True)  125 us
    unnamed x2, blocking collectives  56.5 us
    all_gather x2, blocking collectives, over_axes(): x = jnp.sum(lax.all_gather(x, axis), axis=0)  54.5 us
    all_to_all x2, starting transfers between devices, copy_for_each(): return lax.all_to_all(copies, axis, split_axis=0, concat_axis=0, tiled=True)  39.5 us
    dot_general x8, matrix products, exposure_of(): lax.dot_general(shock_rows, loadings, (((1,), (1,)), ((), ())), preferred...  32 us
    all_to_all x1, blocking collectives, summed_on_arrival(): tiles = lax.all_to_all(cut_along(x, dim, size), axis, 0, 0, tiled=True)  30.4 us
    dot_general x8, matrix products, pnl_one_block(): return jnp.dot(held, table, preferred_element_type=jnp.float32)  23.1 us
    dot_general x8, matrix products, grad_one_block(): lax.dot_general(grad_exposure, shock_block, (((0,), (0,)), ((), ())), pre...  21.1 us
  transfers between devices with their start and end apart: 2, of which 2 were waited for; matrix products, arithmetic and copies ran while one was open for 0% of the time, Pallas kernels for 0%

profile of v1, /device:TPU:37, one launch (start us, length us, event | category | flops | bytes accessed | tf_op | source)
XLA Modules:
  0.0 436.7 jit_solution(2688008372581270954)
XLA Ops:
  3.5 33.2 %all-to-all-start = ((bf16[32,64,256]{2,1,0:T(8,128)(2,1)}), bf16[32,64,256]{2,1,0:T(8,128)(2,1)S(1)}, u32[]{:S(2)}, u32[]{:S(2)}) async-start(bf16[32,64,256]{2,1,0:T(8,128)(2,1)} %broadcast_in_dim.37), calls=%async_computation | async-start | bytes 2097152 | tf_op jit(solution)/shard_map/all_to_all | solution.py:24
  36.8 104.4 %all-to-all-done = bf16[32,64,256]{2,1,0:T(8,128)(2,1)S(1)} async-done(((bf16[32,64,256]{2,1,0:T(8,128)(2,1)}), bf16[32,64,256]{2,1,0:T(8,128)(2,1)S(1)}, u32[]{:S(2)}, u32[]{:S(2)}) %all-to-all-start) | async-done | bytes 1048608 | tf_op jit(solution)/shard_map/all_to_all | solution.py:24
  141.5 6.0 %all_to_all.25 = bf16[2,32,64,256]{3,2,1,0:T(8,128)(2,1)S(1)} all-to-all(bf16[2,32,64,256]{3,2,1,0:T(8,128)(2,1)S(1)} %broadcast_in_dim.38), channel_id=1, replica_groups=mesh['groups'=4,'asset_0'=32,'asset_1'=2] {'asset_1'}, dimensions={0} | all-to-all | bytes 4194304 | tf_op jit(solution)/shard_map/all_to_all | solution.py:24
  149.0 23.3 %while.28 = (s32[]{:T(128)}, f32[8,512,128]{2,1,0:T(8,128)S(1)}, f32[1024]{0:T(1024)S(1)}, bf16[8,512,256]{2,1,0:T(8,128)(2,1)}, bf16[1024,256]{1,0:T(8,128)(2,1...) while((s32[]{:T(128)}, f32[8,512,128]{2,1,0:T(8,128)S(1)}, f32[1024]{0:T(1024)S(1)}, ...), condition=%wide.region_1.2_spmd.clone, body=%wide.region_0.1_spmd.clone.sunk | while | flops 410255360 | bytes 1061981 | solution.py:172
  149.0 2.9 fusion.83
  151.9 2.9 fusion.83
  154.8 2.9 fusion.83
  157.7 2.9 fusion.83
  160.6 2.9 fusion.83
  163.6 2.9 fusion.83
  166.5 2.9 fusion.83
  169.4 2.9 fusion.83
  173.6 30.4 %all_to_all.26 = f32[64,1,128]{2,1,0:T(1,128)S(1)} all-to-all(f32[64,1,128]{2,1,0:T(1,128)S(1)} %bitcast.97), channel_id=1, replica_groups=mesh['groups'=4,'asset_0'=32,'asset_1'=2] {'asset_0','asset_1'}, dimensions={0} | all-to-all | bytes 65536 | tf_op jit(solution)/shard_map/all_to_all | solution.py:45
  204.7 6.3 %all-to-all-start.3 = ((f32[64,1,128]{2,1,0:T(1,128)}), f32[64,1,128]{2,1,0:T(1,128)S(1)}, u32[]{:S(2)}, u32[]{:S(2)}) async-start(f32[64,1,128]{2,1,0:T(1,128)} %broadcast_in_dim.39), calls=%async_computation.3 | async-start | bytes 65536 | tf_op jit(solution)/shard_map/all_to_all | solution.py:24
  212.9 20.7 %all-to-all-done.3 = f32[64,1,128]{2,1,0:T(1,128)S(1)} async-done(((f32[64,1,128]{2,1,0:T(1,128)}), f32[64,1,128]{2,1,0:T(1,128)S(1)}, u32[]{:S(2)}, u32[]{:S(2)}) %all-to-all-start.3) | async-done | bytes 32800 | tf_op jit(solution)/shard_map/all_to_all | solution.py:24
  248.5 65.7 %while.29 = (s32[]{:T(128)}, f32[1024,256]{1,0:T(8,128)S(1)}, f32[1024]{0:T(1024)S(1)}, f32[1024]{0:T(1024)S(1)}, bf16[8,512,128]{2,1,0:T(8,128)(2,1)}, /*index=...) while((s32[]{:T(128)}, f32[1024,256]{1,0:T(8,128)S(1)}, ...), condition=%wide.region_18.19_spmd.clone, body=%wide.region_16.18_spmd.clone.sunk | while | flops 681313280 | bytes 15892648 | solution.py:194
  250.0 4.0 fusion.89
  254.0 2.6 convolution_add_fusion.2
  258.2 4.0 fusion.89
  266.4 4.0 fusion.89
  270.4 2.6 convolution_add_fusion.2
  274.7 4.0 fusion.89
  282.9 4.0 fusion.89
  286.9 2.6 convolution_add_fusion.2
  291.1 4.0 fusion.89
  299.3 4.0 fusion.89
  303.3 2.6 convolution_add_fusion.2
  307.5 4.0 fusion.89
  317.7 39.7 %all-reduce = f32[32]{0:T(128)S(1)} all-reduce(f32[32]{0:T(128)S(1)} %dynamic-update-slice), channel_id=1, replica_groups=mesh['groups'=4,'asset_0'=32,'asset_1'=2] {'asset_0'}, use_global_device_ids=true, to_apply=%add | all-reduce | flops 32 | bytes 256
  361.3 16.8 %all-reduce.1 = f32[2]{0:T(128)S(1)} all-reduce(f32[2]{0:T(128)S(1)} %dynamic-update-slice.1), channel_id=1, replica_groups=mesh['groups'=4,'asset_0'=32,'asset_1'=2] {'asset_1'}, use_global_device_ids=true, to_apply=%add.1 | all-reduce | flops 2 | bytes 16
  381.0 38.5 %all-gather.2 = f32[32,1,128]{2,1,0:T(1,128)S(1)} all-gather(f32[1,1,128]{2,1,0:T(1,128)S(1)} %bitcast.99), channel_id=2, replica_groups=mesh['groups'=4,'asset_0'=32,'asset_1'=2] {'asset_0'}, dimensions={0}, use_global_device_ids=true | all-gather | bytes 16896 | tf_op jit(solution)/shard_map/all_gather | solution.py:65
  419.6 16.0 %all-gather.3 = f32[2,1,128]{2,1,0:T(1,128)S(1)} all-gather(f32[1,1,128]{2,1,0:T(1,128)S(1)} %bitcast.100), channel_id=3, replica_groups=mesh['groups'=4,'asset_0'=32,'asset_1'=2] {'asset_1'}, dimensions={0}, use_global_device_ids=true | all-gather | bytes 1536 | tf_op jit(solution)/shard_map/all_gather | solution.py:65
  (100 shorter events, 51.5 us)
Async XLA Ops:
  0.6 0.9 copy-start
  3.5 137.7 %all-to-all-start = ((bf16[32,64,256]{2,1,0:T(8,128)(2,1)}), bf16[32,64,256]{2,1,0:T(8,128)(2,1)S(1)}, u32[]{:S(2)}, u32[]{:S(2)}) async-start(bf16[32,64,256]{2,1,0:T(8,128)(2,1)} %broadcast_in_dim.37), calls=%async_computation | async-start | bytes 2097152 | tf_op jit(solution)/shard_map/all_to_all | solution.py:24
  147.5 1.4 copy-start.2
  147.5 1.4 copy-start.3
  147.5 1.4 copy-start.4
  147.5 1.4 copy-start.7
  149.0 23.4 %copy-start.6 = (f32[128]{0:T(128)S(1)}, f32[128]{0:T(128)}, u32[]{:S(2)}) copy-start(f32[128]{0:T(128)} %param.19) | copy-start | bytes 1540
  172.3 76.2 %copy-start.1 = (f32[8,512,128]{2,1,0:T(8,128)}, f32[8,512,128]{2,1,0:T(8,128)S(1)}, u32[]{:S(2)}) copy-start(f32[8,512,128]{2,1,0:T(8,128)S(1)} %get-tuple-element.206) | copy-start | bytes 6291460
  172.3 38.7 %copy-start.10 = (u32[256]{0:T(256)S(1)}, u32[256]{0:T(256)}, u32[]{:S(2)}) copy-start(u32[256]{0:T(256)} %constant.96) | copy-start | bytes 3076
  172.3 39.3 %copy-start.9 = (u32[256]{0:T(256)S(1)}, u32[256]{0:T(256)}, u32[]{:S(2)}) copy-start(u32[256]{0:T(256)} %constant.101) | copy-start | bytes 3076
  172.3 63.9 %copy-start.5 = (s32[4096]{0:T(1024)S(1)}, s32[4096]{0:T(1024)}, u32[]{:S(2)}) copy-start(s32[4096]{0:T(1024)} %param.18) | copy-start | bytes 49156
  204.7 28.9 %all-to-all-start.3 = ((f32[64,1,128]{2,1,0:T(1,128)}), f32[64,1,128]{2,1,0:T(1,128)S(1)}, u32[]{:S(2)}, u32[]{:S(2)}) async-start(f32[64,1,128]{2,1,0:T(1,128)} %broadcast_in_dim.39), calls=%async_computation.3 | async-start | bytes 65536 | tf_op jit(solution)/shard_map/all_to_all | solution.py:24
  248.5 1.5 copy-start.8
  256.7 1.5 copy-start.8
  264.9 1.5 copy-start.8
  273.1 1.5 copy-start.8
  281.3 1.5 copy-start.8
  289.6 1.5 copy-start.8
  297.8 1.5 copy-start.8
  306.0 1.5 copy-start.8
